TPU v7x, 32 devices: a whole 2x2x4 slice. The times are simulated.
32 devices in a mesh: grp: 2 (over x), sub: 16 (over z, y, core).
Axes of the slice: x: 2, y: 2, z: 4, core: 2. Of those that a mesh axis runs over, the one named last changes fastest.
Arguments:
- counts: int32 [32], P(('grp', 'sub')), may hold values from 1 to 3, as said below
- block_map: int32 [96], P(('grp', 'sub')), may hold values from 0 to 31
- perms: int32 [96, 256], P(('grp', 'sub')), may hold values from 0 to 255, each once within a row
- mass_ii: bfloat16 [96, 1024, 1024], P(('grp', 'sub')), may hold values from -0.005859375 to 0.005859375
- mass_ib: bfloat16 [96, 1024, 256], P(('grp', 'sub')), may hold values from -0.1875 to 0.1875
- mass_bb: bfloat16 [96, 256, 256], P(('grp', 'sub')), may hold values from -6 to 6
- constraint_modes: bfloat16 [96, 1024, 256], P(('grp', 'sub')), may hold values from -6 to 6
- fixed_modes: bfloat16 [96, 1024, 128], P(('grp', 'sub')), may hold values from -6 to 6
Outputs:
- blocks: float32 [32, 256, 256], P('grp', 'sub')
- coupling: float32 [96, 128, 256], P(('grp', 'sub'))
Inputs may be any that keep to these rules, and one draw needn't show every extreme that they name: `counts`: at least one device uses all 3 slots and one uses a single slot.
All inputs are finite; a program needn't handle non-finite values.
Results may differ from a plain program's by a relative error of at most 0.0021.
Values sent between devices are 32-bit elements; how exact they have to be, the bound alone decides.
A program may use at most 128 MiB of HBM per device.

v0:
```python
import functools

import jax
import jax.numpy as jnp
from jax import lax
from jax.experimental import pallas as pl
from jax.experimental.pallas import tpu as pltpu
from jax.sharding import PartitionSpec as P

NBG = 16
ROWS = 8
LANES = 128
WINDOW = 2
MESH = pl.DeviceIdType.MESH


def split(value):
    high = value.astype(jnp.bfloat16)
    low = (value - high.astype(jnp.float32)).astype(jnp.bfloat16)
    return high, low


def dot(left, right, left_dim=1, right_dim=0):
    return lax.dot_general(
        left,
        right,
        (((left_dim,), (right_dim,)), ((), ())),
        preferred_element_type=jnp.float32,
    )


def send_order(peers):
    return sorted(range(1, peers), key=lambda step: (abs(step - peers // 2), step))


def kernel(
    n_grp,
    n_sub,
    counts,
    codes,
    perms,
    mass_ii,
    mass_ib,
    mass_bb,
    psi_in,
    phi_in,
    blocks,
    coupling,
    m_ii,
    m_bb,
    lhs,
    rhs,
    placed,
    got,
    key_mine,
    key_got,
    hot,
    sums,
    passed,
    in_sem,
    send_sem,
    got_sem,
    key_send_sem,
    key_sem,
    pass_send_sem,
    pass_sem,
):
    grp = lax.axis_index("grp")
    me = lax.axis_index("sub")
    slots, interior, width = psi_in.shape
    chunks = got.shape[0]
    cuts = width // LANES
    own_rows = chunks // cuts * ROWS
    lanes = n_sub * ROWS
    after = lax.rem(grp + 1, n_grp)
    before = lax.rem(grp + n_grp - 1, n_grp)

    def loads(slot):
        pairs = (
            (psi_in, lhs.at[slot, :, pl.ds(0, width)]),
            (mass_ii, m_ii.at[slot]),
            (mass_ib, rhs.at[slot, :, pl.ds(width, width)]),
            (mass_bb, m_bb.at[slot]),
            (phi_in, lhs.at[slot, :, pl.ds(width, lhs.shape[2] - width)]),
        )
        return [
            pltpu.make_async_copy(source.at[slot], held, in_sem.at[slot, index])
            for index, (source, held) in enumerate(pairs)
        ]

    for copy in loads(0):
        copy.start()

    order = send_order(n_sub)
    peers = [lax.rem(me + step, n_sub) for step in order]
    barrier = pltpu.get_barrier_semaphore()
    for peer in peers:
        pl.semaphore_signal(barrier, inc=1, device_id=(grp, peer), device_id_type=MESH)
    pl.semaphore_signal(barrier, inc=1, device_id=(after, me), device_id_type=MESH)
    greeted = len(peers) + 1
    if n_grp > 2:
        pl.semaphore_signal(barrier, inc=1, device_id=(before, me), device_id_type=MESH)
        greeted += 1

    lane = lax.broadcasted_iota(jnp.int32, (1, lanes), 1)
    key_mine[...] = jnp.zeros_like(key_mine)
    for slot in range(slots):
        code = jnp.where(slot < counts[0], codes[slot] * ROWS, -2 * NBG * ROWS)
        key_mine[slot : slot + 1, :] = jnp.where(lane // ROWS == me, code + lane % ROWS, 0)
    key_got[pl.ds(me, 1)] = key_mine[...][None]

    def key_copy(peer):
        return pltpu.make_async_remote_copy(
            src_ref=key_mine,
            dst_ref=key_got.at[me],
            send_sem=key_send_sem,
            recv_sem=key_sem,
            device_id=(grp, peer),
            device_id_type=MESH,
        )

    def send(chunk, slot):
        for peer in peers:
            top = pl.multiple_of(peer * own_rows + chunk // cuts * ROWS, ROWS)
            left = chunk % cuts * LANES
            pltpu.make_async_remote_copy(
                src_ref=placed.at[slot, pl.ds(top, ROWS), pl.ds(left, LANES)],
                dst_ref=got.at[chunk, slot, me],
                send_sem=send_sem.at[chunk, slot],
                recv_sem=got_sem.at[chunk, slot],
                device_id=(grp, peer),
                device_id_type=MESH,
            ).start()

    @pl.loop(0, slots)
    def one_slot(slot):
        copies = loads(slot)

        @pl.when(slot + 1 < slots)
        def ahead_loads():
            for copy in loads(slot + 1):
                copy.start()

        copies[0].wait()
        copies[1].wait()
        step = min(interior, 256)
        modes = lhs[slot, :, :width]
        for top in range(0, interior, step):
            made = dot(m_ii[slot, top : top + step, :], modes).astype(jnp.bfloat16)
            rhs[slot, top : top + step, :width] = made
        for copy in copies[2:]:
            copy.wait()
        every = dot(lhs[slot], rhs[slot], 0, 0)
        cross = every[:width, width:]
        direct = every[:width, :width] + cross + m_bb[slot].astype(jnp.float32)
        place = lax.broadcasted_iota(jnp.int32, (width, width), 0)
        pick = jnp.where(place == perms[pl.ds(slot, 1), :], 1.0, 0.0).astype(jnp.bfloat16)
        high, low = split(direct)
        cross_high, cross_low = split(cross)
        rows = dot(pick, high) + dot(pick, low)
        rows = rows + dot(pick, cross_high, 1, 1) + dot(pick, cross_low, 1, 1)
        high, low = split(rows)
        placed[slot] = dot(high, pick, 1, 1) + dot(low, pick, 1, 1)
        active = jnp.where(slot < counts[0], 1.0, 0.0)
        coupling[slot] = (every[width:, :width] + every[width:, width:]) * active
        for chunk in range(chunks):
            mine = pl.multiple_of(me * own_rows + chunk // cuts * ROWS, ROWS)
            left = chunk % cuts * LANES
            own = placed[slot, pl.ds(mine, ROWS), left : left + LANES]
            got[chunk, slot, pl.ds(me, 1)] = own[None]

        @pl.when(slot == 0)
        def enter():
            pl.semaphore_wait(barrier, greeted)
            for peer in peers:
                key_copy(peer).start()

        @pl.when(slot < slots - 1)
        def spread():
            for chunk in range(chunks):
                send(chunk, slot)

    window = min(WINDOW, chunks)
    for chunk in range(window):
        send(chunk, slots - 1)

    many = n_sub - 1
    all_keys = key_got.at[pl.ds(0, many)]
    pltpu.make_async_copy(all_keys, all_keys, key_sem).wait()
    keys = jnp.sum(key_got[...], axis=0)
    target = lax.broadcasted_iota(jnp.int32, (2 * NBG * ROWS, lanes), 0)
    for slot in range(slots):
        hot[slot] = jnp.where(target == keys[slot : slot + 1, :], 1.0, 0.0).astype(jnp.bfloat16)

    def pass_copy(chunk):
        return pltpu.make_async_remote_copy(
            src_ref=sums.at[chunk, pl.ds(NBG * ROWS, NBG * ROWS)],
            dst_ref=passed.at[chunk],
            send_sem=pass_send_sem.at[chunk],
            recv_sem=pass_sem.at[chunk],
            device_id=(after, me),
            device_id_type=MESH,
        )

    def owner_sum(chunk, slot):
        arrived = got.at[chunk, slot, pl.ds(0, many)]
        pltpu.make_async_copy(arrived, arrived, got_sem.at[chunk, slot]).wait()
        high, low = split(got[chunk, slot].reshape(lanes, LANES))
        return dot(hot[slot], high) + dot(hot[slot], low)

    for slot in range(slots):
        for chunk in range(chunks):
            total = owner_sum(chunk, slot)
            if slot > 0:
                total = total + sums[chunk]
            sums[chunk] = total
            if slot == slots - 1:
                pass_copy(chunk).start()
                if chunk + window < chunks:
                    send(chunk + window, slot)

    for chunk in range(chunks):
        pass_copy(chunk).wait()
        own = sums[chunk, : NBG * ROWS] + passed[chunk]
        top, left = chunk // cuts * ROWS, chunk % cuts * LANES
        blocks[:, top : top + ROWS, left : left + LANES] = own.reshape(NBG, ROWS, LANES)

    pltpu.make_async_copy(all_keys, all_keys, key_send_sem).wait()
    for chunk in range(chunks):
        for slot in range(slots):
            arrived = got.at[chunk, slot, pl.ds(0, many)]
            pltpu.make_async_copy(arrived, arrived, send_sem.at[chunk, slot]).wait()


def halves_kernel(
    n_grp,
    n_sub,
    counts,
    codes,
    perms,
    mass_ii,
    mass_ib,
    mass_bb,
    psi_in,
    phi_in,
    blocks,
    coupling,
    m_ii,
    m_bb,
    lhs,
    rhs,
    placed,
    got,
    key_mine,
    key_got,
    hot,
    sums,
    passed,
    in_sem,
    send_sem,
    got_sem,
    key_send_sem,
    key_sem,
    pass_send_sem,
    pass_sem,
):
    grp = lax.axis_index("grp")
    me = lax.axis_index("sub")
    slots, interior, width = psi_in.shape
    own_rows = width // n_sub
    half = n_sub // 2
    lanes = n_sub * ROWS
    part_rows = NBG * ROWS
    other = 1 - grp
    far = lax.rem(me + half, n_sub)
    member = grp * half + lax.rem(me, half)
    first = me - lax.rem(me, half)

    def loads(slot):
        pairs = (
            (psi_in, lhs.at[slot, :, pl.ds(0, width)]),
            (mass_ii, m_ii.at[slot]),
            (mass_ib, rhs.at[slot, :, pl.ds(width, width)]),
            (mass_bb, m_bb.at[slot]),
            (phi_in, lhs.at[slot, :, pl.ds(width, lhs.shape[2] - width)]),
        )
        return [
            pltpu.make_async_copy(source.at[slot], held, in_sem.at[slot, index])
            for index, (source, held) in enumerate(pairs)
        ]

    for copy in loads(0):
        copy.start()

    peers = []
    for step in send_order(n_sub):
        index = lax.rem(member + step, n_sub)
        peers.append((index // half, first + lax.rem(index, half)))
    barrier = pltpu.get_barrier_semaphore()
    for peer in peers + [(grp, far), (other, far)]:
        pl.semaphore_signal(barrier, inc=1, device_id=peer, device_id_type=MESH)
    greeted = len(peers) + 2

    lane = lax.broadcasted_iota(jnp.int32, (1, lanes), 1)
    key_mine[...] = jnp.zeros_like(key_mine)
    for slot in range(slots):
        code = codes[slot]
        block = lax.rem(grp + code // NBG, n_grp) * NBG + lax.rem(code, NBG)
        block = jnp.where(slot < counts[0], block, -n_grp * NBG) * ROWS
        key_mine[slot : slot + 1, :] = jnp.where(lane // ROWS == member, block + lane % ROWS, 0)
    key_got[pl.ds(member, 1)] = key_mine[...][None]

    def key_copy(peer):
        return pltpu.make_async_remote_copy(
            src_ref=key_mine,
            dst_ref=key_got.at[member],
            send_sem=key_send_sem,
            recv_sem=key_sem,
            device_id=peer,
            device_id_type=MESH,
        )

    def row_of(part, peer):
        owner = lax.rem(peer[1] + half, n_sub) if part == 0 else peer[1]
        return pl.multiple_of(owner * own_rows + peer[0] * ROWS, ROWS)

    def send(part, slot):
        for peer in peers:
            pltpu.make_async_remote_copy(
                src_ref=placed.at[slot, pl.ds(row_of(part, peer), ROWS), :],
                dst_ref=got.at[part, slot, member],
                send_sem=send_sem.at[part, slot],
                recv_sem=got_sem.at[part, slot],
                device_id=peer,
                device_id_type=MESH,
            ).start()

    @pl.loop(0, slots)
    def one_slot(slot):
        copies = loads(slot)

        @pl.when(slot + 1 < slots)
        def ahead_loads():
            for copy in loads(slot + 1):
                copy.start()

        copies[0].wait()
        copies[1].wait()
        step = min(interior, 256)
        modes = lhs[slot, :, :width]
        for top in range(0, interior, step):
            made = dot(m_ii[slot, top : top + step, :], modes).astype(jnp.bfloat16)
            rhs[slot, top : top + step, :width] = made
        for copy in copies[2:]:
            copy.wait()
        every = dot(lhs[slot], rhs[slot], 0, 0)
        cross = every[:width, width:]
        direct = every[:width, :width] + cross + m_bb[slot].astype(jnp.float32)
        place = lax.broadcasted_iota(jnp.int32, (width, width), 0)
        pick = jnp.where(place == perms[pl.ds(slot, 1), :], 1.0, 0.0).astype(jnp.bfloat16)
        high, low = split(direct)
        cross_high, cross_low = split(cross)
        rows = dot(pick, high) + dot(pick, low)
        rows = rows + dot(pick, cross_high, 1, 1) + dot(pick, cross_low, 1, 1)
        high, low = split(rows)
        placed[slot] = dot(high, pick, 1, 1) + dot(low, pick, 1, 1)
        active = jnp.where(slot < counts[0], 1.0, 0.0)
        coupling[slot] = (every[width:, :width] + every[width:, width:]) * active
        for part in range(2):
            own = placed[slot, pl.ds(row_of(part, (grp, me)), ROWS), :]
            got[part, slot, pl.ds(member, 1)] = own[None]

        @pl.when(slot == 0)
        def enter():
            pl.semaphore_wait(barrier, greeted)
            for peer in peers:
                key_copy(peer).start()

        send(0, slot)

    for slot in range(slots):
        send(1, slot)

    many = n_sub - 1
    all_keys = key_got.at[pl.ds(0, many)]
    pltpu.make_async_copy(all_keys, all_keys, key_sem).wait()
    keys = jnp.sum(key_got[...], axis=0)
    target = lax.broadcasted_iota(jnp.int32, (2 * NBG * ROWS, lanes), 0)
    for slot in range(slots):
        hot[slot] = jnp.where(target == keys[slot : slot + 1, :], 1.0, 0.0).astype(jnp.bfloat16)

    def pass_copy(source, part, place, peer):
        return pltpu.make_async_remote_copy(
            src_ref=sums.at[source, pl.ds(pl.multiple_of(part * part_rows, part_rows), part_rows)],
            dst_ref=passed.at[place],
            send_sem=pass_send_sem.at[source],
            recv_sem=pass_sem.at[place],
            device_id=peer,
            device_id_type=MESH,
        )

    def owner_sum(part):
        total = None
        for slot in range(slots):
            arrived = got.at[part, slot, pl.ds(0, many)]
            pltpu.make_async_copy(arrived, arrived, got_sem.at[part, slot]).wait()
            high, low = split(got[part, slot].reshape(lanes, width))
            one = dot(hot[slot], high) + dot(hot[slot], low)
            total = one if total is None else total + one
        sums[part] = total

    owner_sum(0)
    pass_copy(0, other, grp, (other, far)).start()
    pass_copy(0, grp, grp, (grp, far)).start()
    owner_sum(1)
    pass_copy(1, other, 2, (other, me)).start()

    pltpu.make_async_copy(all_keys, all_keys, key_send_sem).wait()
    for part in range(2):
        for slot in range(slots):
            arrived = got.at[part, slot, pl.ds(0, many)]
            pltpu.make_async_copy(arrived, arrived, send_sem.at[part, slot]).wait()

    for place in range(3):
        pltpu.make_async_copy(passed.at[place], passed.at[place], pass_sem.at[place]).wait()
    kept = sums[1, pl.ds(pl.multiple_of(grp * part_rows, part_rows), part_rows), :]
    for row, near in ((grp, kept), (other, passed[2])):
        value = (passed[row] + near).reshape(NBG, ROWS, width)
        blocks[:, pl.ds(pl.multiple_of(row * ROWS, ROWS), ROWS), :] = value

    both = sums.at[0]
    pltpu.make_async_copy(both, both, pass_send_sem.at[0]).wait()
    pltpu.make_async_copy(passed.at[2], passed.at[2], pass_send_sem.at[1]).wait()


def per_device(n_grp, n_sub, counts, block_map, perms, mass_ii, mass_ib, mass_bb, psi, phi):
    slots, interior, width = psi.shape
    modes = phi.shape[2]
    own_rows = width // n_sub
    chunks = own_rows // ROWS * (width // LANES)
    cut = LANES
    lanes = n_sub * ROWS
    body = kernel
    places = chunks
    if n_grp == 2 and own_rows == 2 * ROWS and n_sub % 2 == 0:
        body, chunks, places, cut = halves_kernel, 2, 3, width
    key_rows = -(-slots // 8) * 8
    smem = pl.BlockSpec(memory_space=pltpu.SMEM)
    vmem = pl.BlockSpec(memory_space=pltpu.VMEM)
    hbm = pl.BlockSpec(memory_space=pl.ANY)
    bf16, f32, i32 = jnp.bfloat16, jnp.float32, jnp.int32
    dma = pltpu.SemaphoreType.DMA
    return pl.pallas_call(
        functools.partial(body, n_grp, n_sub),
        out_shape=(
            pltpu.VMEM((NBG, own_rows, width), f32),
            pltpu.VMEM((slots, modes, width), f32),
        ),
        in_specs=[smem, smem, vmem] + [hbm] * 5,
        out_specs=(vmem, vmem),
        scratch_shapes=[
            pltpu.VMEM(mass_ii.shape, bf16),
            pltpu.VMEM(mass_bb.shape, bf16),
            pltpu.VMEM((slots, interior, width + modes), bf16),
            pltpu.VMEM((slots, interior, 2 * width), bf16),
            pltpu.VMEM((slots, width, width), f32),
            pltpu.VMEM((chunks, slots, n_sub, ROWS, cut), f32),
            pltpu.VMEM((key_rows, lanes), i32),
            pltpu.VMEM((n_sub, key_rows, lanes), i32),
            pltpu.VMEM((slots, 2 * NBG * ROWS, lanes), bf16),
            pltpu.VMEM((chunks, 2 * NBG * ROWS, cut), f32),
            pltpu.VMEM((places, NBG * ROWS, cut), f32),
            dma((slots, 5)),
            dma((chunks, slots)),
            dma((chunks, slots)),
            dma,
            dma,
            dma((chunks,)),
            dma((places,)),
        ],
        compiler_params=pltpu.CompilerParams(
            collective_id=0, has_side_effects=True, vmem_limit_bytes=56 * 1024 * 1024
        ),
    )(counts, block_map, perms, mass_ii, mass_ib, mass_bb, psi, phi)


def solution(mesh):
    both = P(("grp", "sub"))
    return jax.shard_map(
        functools.partial(per_device, mesh.shape["grp"], mesh.shape["sub"]),
        mesh=mesh,
        in_specs=(both,) * 8,
        out_specs=(P("grp", "sub", None), both),
        check_vma=False,
    )
```

profile of v0, /device:TPU:0, one launch (start us, length us, event | category | flops | bytes accessed | tf_op | source)
XLA Modules:
  0.0 34.5 jit_solution(5465119766254771218)
XLA Ops:
  1.3 31.8 %shard_map.95 = (f32[16,16,256]{2,1,0:T(8,128)S(1)}, f32[3,128,256]{2,1,0:T(8,128)S(1)}) custom-call(s32[1]{0:T(128)S(6)} %copy.14.counts, s32[3]{0:T(128)} %codes.1, s32[3,256]{1,0:T(4,128)} %perms.1, bf16[3,1024,1024]{2,1,0:T(8,128)(2,1)} %mass_ii.1, bf16[3,1024,256]{2,1,0:T(8,128)(2,1)} %mass_ib.1, bf16[3,256,256]{2,1,0:T(8,128)(2,1)} %mass_bb.1, ...), custom_call_target="tpu_custom_call" | custom-call | tf_op jit(solution)/shard_map/pallas_call | solution.py:453
  33.0 0.7 %copy.12 = f32[16,16,256]{2,1,0:T(8,128)} copy(f32[16,16,256]{2,1,0:T(8,128)S(1)} %get-tuple-element.2) | data formatting | bytes 524288
  33.8 0.7 %copy.13 = f32[3,128,256]{2,1,0:T(8,128)} copy(f32[3,128,256]{2,1,0:T(8,128)S(1)} %get-tuple-element.3) | data formatting | bytes 786432
where the time goes:
time: 34.7 us; the launch traced here: 34.5 us
  Pallas kernels  31.8 us (92%)
  local copies, waits for them, and re-layouts  1.45 us (4%)
  between operations  1.29 us (4%)
    pallas_call x1, Pallas kernels, per_device(): pl.pallas_call(functools.partial(body, n_grp, n_sub), out_shape=(pltpu.VM...  31.8 us
    unnamed x2, local copies, waits for them, and re-layouts  1.45 us

commit v1 on v0

--- a/solution.py
+++ b/solution.py
@@ -11,6 +11,7 @@
 ROWS = 8
 LANES = 128
 WINDOW = 2
+STRIPS = 4
 MESH = pl.DeviceIdType.MESH
 
 
@@ -232,7 +233,7 @@
             pltpu.make_async_copy(arrived, arrived, send_sem.at[chunk, slot]).wait()
 
 
-def halves_kernel(
+def cross_kernel(
     n_grp,
     n_sub,
     counts,
@@ -250,12 +251,16 @@
     lhs,
     rhs,
     placed,
-    got,
+    near,
+    far,
+    held,
     key_mine,
     key_got,
     hot,
     sums,
+    part,
     passed,
+    landed,
     in_sem,
     send_sem,
     got_sem,
@@ -271,10 +276,16 @@
     half = n_sub // 2
     lanes = n_sub * ROWS
     part_rows = NBG * ROWS
+    cut = width // 2
+    quad = half // 2
     other = 1 - grp
-    far = lax.rem(me + half, n_sub)
-    member = grp * half + lax.rem(me, half)
-    first = me - lax.rem(me, half)
+    spot = lax.rem(me, half)
+    first = me - spot
+    beyond = half - first
+    twin = beyond + spot
+    member = grp * half + spot
+    reach = grp + me // quad + lax.rem(me // 2, 2)
+    gate = jnp.maximum(slots - 1 - reach, 0)
 
     def loads(slot):
         pairs = (
@@ -285,74 +296,113 @@
             (phi_in, lhs.at[slot, :, pl.ds(width, lhs.shape[2] - width)]),
         )
         return [
-            pltpu.make_async_copy(source.at[slot], held, in_sem.at[slot, index])
-            for index, (source, held) in enumerate(pairs)
+            pltpu.make_async_copy(source.at[slot], into, in_sem.at[slot, index])
+            for index, (source, into) in enumerate(pairs)
         ]
 
-    for copy in loads(0):
-        copy.start()
-
-    peers = []
-    for step in send_order(n_sub):
-        index = lax.rem(member + step, n_sub)
-        peers.append((index // half, first + lax.rem(index, half)))
+    for slot in range(slots):
+        for copy in loads(slot):
+            copy.start()
+
+    def peer_at(base, plane, turn, step):
+        low = plane * quad + lax.rem(me + step, quad)
+        return lax.rem(grp + turn, n_grp), base + low
+
+    steps = [(1, 2), (0, 2), (1, 3), (0, 3), (1, 1), (1, 0), (0, 1), (0, 0)]
+    across = [peer_at(beyond, plane, *step) for plane in range(2) for step in steps]
+    close = [
+        (peer_at(first, plane, *step), None if step != (0, 0) else spot // quad != plane)
+        for plane in range(2)
+        for step in steps
+    ]
     barrier = pltpu.get_barrier_semaphore()
-    for peer in peers + [(grp, far), (other, far)]:
+
+    def greet(peer):
         pl.semaphore_signal(barrier, inc=1, device_id=peer, device_id_type=MESH)
-    greeted = len(peers) + 2
+
+    def each_close(act):
+        for peer, other_one in close:
+            if other_one is None:
+                act(peer)
+            else:
+                pl.when(other_one)(functools.partial(act, peer))
+
+    for peer in across:
+        greet(peer)
+    each_close(greet)
 
     lane = lax.broadcasted_iota(jnp.int32, (1, lanes), 1)
-    key_mine[...] = jnp.zeros_like(key_mine)
     for slot in range(slots):
         code = codes[slot]
         block = lax.rem(grp + code // NBG, n_grp) * NBG + lax.rem(code, NBG)
         block = jnp.where(slot < counts[0], block, -n_grp * NBG) * ROWS
-        key_mine[slot : slot + 1, :] = jnp.where(lane // ROWS == member, block + lane % ROWS, 0)
-    key_got[pl.ds(member, 1)] = key_mine[...][None]
-
-    def key_copy(peer):
-        return pltpu.make_async_remote_copy(
-            src_ref=key_mine,
-            dst_ref=key_got.at[member],
-            send_sem=key_send_sem,
-            recv_sem=key_sem,
+        key_mine[slot] = jnp.where(lane // ROWS == member, block + lane % ROWS, 0)
+    key_got[0, pl.ds(member, 1)] = key_mine[...][None]
+
+    def row_of(peer, owner):
+        return pl.multiple_of(owner * own_rows + peer[0] * ROWS, ROWS)
+
+    def push(source, into, kind, slot, peer):
+        pltpu.make_async_remote_copy(
+            src_ref=source,
+            dst_ref=into,
+            send_sem=send_sem.at[kind, slot],
+            recv_sem=got_sem.at[kind, slot],
             device_id=peer,
             device_id_type=MESH,
-        )
-
-    def row_of(part, peer):
-        owner = lax.rem(peer[1] + half, n_sub) if part == 0 else peer[1]
-        return pl.multiple_of(owner * own_rows + peer[0] * ROWS, ROWS)
-
-    def send(part, slot):
-        for peer in peers:
+        ).start()
+
+    def send_keys():
+        def key_copy(side, peer):
             pltpu.make_async_remote_copy(
-                src_ref=placed.at[slot, pl.ds(row_of(part, peer), ROWS), :],
-                dst_ref=got.at[part, slot, member],
-                send_sem=send_sem.at[part, slot],
-                recv_sem=got_sem.at[part, slot],
+                src_ref=key_mine,
+                dst_ref=key_got.at[side, member],
+                send_sem=key_send_sem.at[side],
+                recv_sem=key_sem.at[side],
                 device_id=peer,
                 device_id_type=MESH,
             ).start()
 
-    @pl.loop(0, slots)
-    def one_slot(slot):
-        copies = loads(slot)
-
-        @pl.when(slot + 1 < slots)
-        def ahead_loads():
-            for copy in loads(slot + 1):
-                copy.start()
-
-        copies[0].wait()
-        copies[1].wait()
-        step = min(interior, 256)
+        for peer in across:
+            key_copy(1, peer)
+        each_close(functools.partial(key_copy, 0))
+
+    def send_far(slot):
+        for peer in across:
+            rows = pl.ds(row_of(peer, peer[1]), ROWS)
+            push(placed.at[slot, rows, pl.ds(0, cut)], far.at[slot, member], 0, slot, peer)
+
+    def held_rows(peer):
+        return pl.ds(row_of(peer, beyond + peer[1] - first), ROWS)
+
+    def send_held(slot):
+        def one(peer):
+            source = placed.at[slot, held_rows(peer), pl.ds(cut, cut)]
+            push(source, held.at[slot, member], 1, slot, peer)
+
+        each_close(one)
+
+    def send_near(slot):
+        def one(peer):
+            rows = pl.ds(row_of(peer, peer[1]), ROWS)
+            push(placed.at[slot, rows, :], near.at[slot, member], 2, slot, peer)
+
+        each_close(one)
+
+    def spread(slot):
+        send_far(slot)
+        send_held(slot)
+        if slot > 0:
+            send_near(slot - 1)
+
+    def reduce_slot(slot):
+        for copy in loads(slot):
+            copy.wait()
         modes = lhs[slot, :, :width]
+        step = interior // STRIPS
         for top in range(0, interior, step):
             made = dot(m_ii[slot, top : top + step, :], modes).astype(jnp.bfloat16)
             rhs[slot, top : top + step, :width] = made
-        for copy in copies[2:]:
-            copy.wait()
         every = dot(lhs[slot], rhs[slot], 0, 0)
         cross = every[:width, width:]
         direct = every[:width, :width] + cross + m_bb[slot].astype(jnp.float32)
@@ -366,71 +416,136 @@
         placed[slot] = dot(high, pick, 1, 1) + dot(low, pick, 1, 1)
         active = jnp.where(slot < counts[0], 1.0, 0.0)
         coupling[slot] = (every[width:, :width] + every[width:, width:]) * active
-        for part in range(2):
-            own = placed[slot, pl.ds(row_of(part, (grp, me)), ROWS), :]
-            got[part, slot, pl.ds(member, 1)] = own[None]
-
-        @pl.when(slot == 0)
+        mine = pl.ds(row_of((grp, me), me), ROWS)
+        near[slot, pl.ds(member, 1)] = placed[slot, mine, :][None]
+        mine = pl.ds(row_of((grp, me), twin), ROWS)
+        held[slot, pl.ds(member, 1)] = placed[slot, mine, pl.ds(cut, cut)][None]
+
+    for slot in range(slots):
+        reduce_slot(slot)
+
+        @pl.when(gate == slot)
         def enter():
-            pl.semaphore_wait(barrier, greeted)
-            for peer in peers:
-                key_copy(peer).start()
-
-        send(0, slot)
-
-    for slot in range(slots):
-        send(1, slot)
+            pl.semaphore_wait(barrier, 2 * n_sub - 1)
+            send_keys()
+            for early in range(slot):
+                spread(early)
+
+        @pl.when(gate <= slot)
+        def follow():
+            spread(slot)
+
+    send_near(slots - 1)
 
     many = n_sub - 1
-    all_keys = key_got.at[pl.ds(0, many)]
-    pltpu.make_async_copy(all_keys, all_keys, key_sem).wait()
-    keys = jnp.sum(key_got[...], axis=0)
-    target = lax.broadcasted_iota(jnp.int32, (2 * NBG * ROWS, lanes), 0)
-    for slot in range(slots):
-        hot[slot] = jnp.where(target == keys[slot : slot + 1, :], 1.0, 0.0).astype(jnp.bfloat16)
-
-    def pass_copy(source, part, place, peer):
+
+    def settle(ref, sem):
+        pltpu.make_async_copy(ref, ref, sem).wait()
+
+    settle(key_got.at[0, pl.ds(0, many)], key_sem.at[0])
+    settle(key_got.at[1], key_sem.at[1])
+    target = lax.broadcasted_iota(jnp.int32, (n_grp * part_rows, lanes), 0)
+    for side in range(2):
+        keys = jnp.sum(key_got[side], axis=0)
+        for slot in range(slots):
+            hot[side, slot] = jnp.where(target == keys[slot], 1.0, 0.0).astype(jnp.bfloat16)
+
+    def gather(side, slot, got):
+        high, low = split(got.reshape(lanes, got.shape[-1]))
+        return dot(hot[side, slot], high) + dot(hot[side, slot], low)
+
+    total = None
+    for slot in range(slots):
+        settle(held.at[slot, pl.ds(0, many)], got_sem.at[1, slot])
+        one = gather(0, slot, held[slot])
+        total = one if total is None else total + one
+    part[...] = total
+
+    def hand(to):
         return pltpu.make_async_remote_copy(
-            src_ref=sums.at[source, pl.ds(pl.multiple_of(part * part_rows, part_rows), part_rows)],
-            dst_ref=passed.at[place],
-            send_sem=pass_send_sem.at[source],
-            recv_sem=pass_sem.at[place],
-            device_id=peer,
+            src_ref=part.at[pl.ds(pl.multiple_of(to * part_rows, part_rows), part_rows)],
+            dst_ref=landed.at[grp],
+            send_sem=pass_send_sem.at[0],
+            recv_sem=pass_sem.at[grp],
+            device_id=(to, twin),
             device_id_type=MESH,
         )
 
-    def owner_sum(part):
-        total = None
-        for slot in range(slots):
-            arrived = got.at[part, slot, pl.ds(0, many)]
-            pltpu.make_async_copy(arrived, arrived, got_sem.at[part, slot]).wait()
-            high, low = split(got[part, slot].reshape(lanes, width))
-            one = dot(hot[slot], high) + dot(hot[slot], low)
-            total = one if total is None else total + one
-        sums[part] = total
-
-    owner_sum(0)
-    pass_copy(0, other, grp, (other, far)).start()
-    pass_copy(0, grp, grp, (grp, far)).start()
-    owner_sum(1)
-    pass_copy(1, other, 2, (other, me)).start()
-
-    pltpu.make_async_copy(all_keys, all_keys, key_send_sem).wait()
-    for part in range(2):
-        for slot in range(slots):
-            arrived = got.at[part, slot, pl.ds(0, many)]
-            pltpu.make_async_copy(arrived, arrived, send_sem.at[part, slot]).wait()
-
-    for place in range(3):
-        pltpu.make_async_copy(passed.at[place], passed.at[place], pass_sem.at[place]).wait()
-    kept = sums[1, pl.ds(pl.multiple_of(grp * part_rows, part_rows), part_rows), :]
-    for row, near in ((grp, kept), (other, passed[2])):
-        value = (passed[row] + near).reshape(NBG, ROWS, width)
-        blocks[:, pl.ds(pl.multiple_of(row * ROWS, ROWS), ROWS), :] = value
-
-    both = sums.at[0]
-    pltpu.make_async_copy(both, both, pass_send_sem.at[0]).wait()
-    pltpu.make_async_copy(passed.at[2], passed.at[2], pass_send_sem.at[1]).wait()
+    hand(other).start()
+    hand(grp).start()
+
+    total = None
+    for slot in range(slots):
+        settle(near.at[slot, pl.ds(0, many)], got_sem.at[2, slot])
+        one = gather(0, slot, near[slot])
+        total = one if total is None else total + one
+    sums[...] = total
+    total = None
+    for slot in range(slots):
+        settle(far.at[slot], got_sem.at[0, slot])
+        one = gather(1, slot, far[slot])
+        total = one if total is None else total + one
+    sums[:, :cut] = sums[:, :cut] + total
+    swap = pltpu.make_async_remote_copy(
+        src_ref=sums.at[pl.ds(pl.multiple_of(other * part_rows, part_rows), part_rows)],
+        dst_ref=passed,
+        send_sem=pass_send_sem.at[1],
+        recv_sem=pass_sem.at[2],
+        device_id=(other, me),
+        device_id_type=MESH,
+    )
+    swap.start()
+
+    settle(key_got.at[0, pl.ds(0, many)], key_send_sem.at[0])
+    settle(key_got.at[1], key_send_sem.at[1])
+    for slot in range(slots):
+        settle(far.at[slot], send_sem.at[0, slot])
+        settle(held.at[slot, pl.ds(0, many)], send_sem.at[1, slot])
+        settle(near.at[slot, pl.ds(0, many)], send_sem.at[2, slot])
+
+    kept = sums[pl.ds(pl.multiple_of(grp * part_rows, part_rows), part_rows), :]
+    swap.wait()
+    for row, value in ((grp, kept), (other, passed[...])):
+        into = pl.ds(pl.multiple_of(row * ROWS, ROWS), ROWS)
+        blocks[:, into, :cut] = value[:, :cut].reshape(NBG, ROWS, cut)
+    settle(landed.at[0], pass_sem.at[0])
+    settle(landed.at[1], pass_sem.at[1])
+    for row, value in ((grp, kept), (other, passed[...])):
+        into = pl.ds(pl.multiple_of(row * ROWS, ROWS), ROWS)
+        late = value[:, cut:] + landed[row]
+        blocks[:, into, cut:] = late.reshape(NBG, ROWS, cut)
+    settle(landed, pass_send_sem.at[0])
+
+
+def cross_scratch(n_grp, n_sub, slots, interior, width, modes):
+    bf16, f32, i32 = jnp.bfloat16, jnp.float32, jnp.int32
+    dma = pltpu.SemaphoreType.DMA
+    lanes, cut = n_sub * ROWS, width // 2
+    total = n_grp * NBG * ROWS
+    return [
+        pltpu.VMEM((slots, interior, interior), bf16),
+        pltpu.VMEM((slots, width, width), bf16),
+        pltpu.VMEM((slots, interior, width + modes), bf16),
+        pltpu.VMEM((slots, interior, 2 * width), bf16),
+        pltpu.VMEM((slots, width, width), f32),
+        pltpu.VMEM((slots, n_sub, ROWS, width), f32),
+        pltpu.VMEM((slots, n_sub, ROWS, cut), f32),
+        pltpu.VMEM((slots, n_sub, ROWS, cut), f32),
+        pltpu.VMEM((slots, 1, lanes), i32),
+        pltpu.VMEM((2, n_sub, slots, 1, lanes), i32),
+        pltpu.VMEM((2, slots, total, lanes), bf16),
+        pltpu.VMEM((total, width), f32),
+        pltpu.VMEM((total, cut), f32),
+        pltpu.VMEM((NBG * ROWS, width), f32),
+        pltpu.VMEM((n_grp, NBG * ROWS, cut), f32),
+        dma((slots, 5)),
+        dma((3, slots)),
+        dma((3, slots)),
+        dma((2,)),
+        dma((2,)),
+        dma((2,)),
+        dma((3,)),
+    ]
 
 
 def per_device(n_grp, n_sub, counts, block_map, perms, mass_ii, mass_ib, mass_bb, psi, phi):
@@ -438,18 +553,38 @@
     modes = phi.shape[2]
     own_rows = width // n_sub
     chunks = own_rows // ROWS * (width // LANES)
-    cut = LANES
     lanes = n_sub * ROWS
     body = kernel
-    places = chunks
-    if n_grp == 2 and own_rows == 2 * ROWS and n_sub % 2 == 0:
-        body, chunks, places, cut = halves_kernel, 2, 3, width
+    fits = n_grp == 2 and n_sub * ROWS == LANES and own_rows == 2 * ROWS and width == 2 * LANES
     key_rows = -(-slots // 8) * 8
     smem = pl.BlockSpec(memory_space=pltpu.SMEM)
     vmem = pl.BlockSpec(memory_space=pltpu.VMEM)
     hbm = pl.BlockSpec(memory_space=pl.ANY)
     bf16, f32, i32 = jnp.bfloat16, jnp.float32, jnp.int32
     dma = pltpu.SemaphoreType.DMA
+    scratch = [
+        pltpu.VMEM(mass_ii.shape, bf16),
+        pltpu.VMEM(mass_bb.shape, bf16),
+        pltpu.VMEM((slots, interior, width + modes), bf16),
+        pltpu.VMEM((slots, interior, 2 * width), bf16),
+        pltpu.VMEM((slots, width, width), f32),
+        pltpu.VMEM((chunks, slots, n_sub, ROWS, LANES), f32),
+        pltpu.VMEM((key_rows, lanes), i32),
+        pltpu.VMEM((n_sub, key_rows, lanes), i32),
+        pltpu.VMEM((slots, 2 * NBG * ROWS, lanes), bf16),
+        pltpu.VMEM((chunks, 2 * NBG * ROWS, LANES), f32),
+        pltpu.VMEM((chunks, NBG * ROWS, LANES), f32),
+        dma((slots, 5)),
+        dma((chunks, slots)),
+        dma((chunks, slots)),
+        dma,
+        dma,
+        dma((chunks,)),
+        dma((chunks,)),
+    ]
+    if fits and interior % STRIPS == 0:
+        body = cross_kernel
+        scratch = cross_scratch(n_grp, n_sub, slots, interior, width, modes)
     return pl.pallas_call(
         functools.partial(body, n_grp, n_sub),
         out_shape=(
@@ -458,26 +593,7 @@
         ),
         in_specs=[smem, smem, vmem] + [hbm] * 5,
         out_specs=(vmem, vmem),
-        scratch_shapes=[
-            pltpu.VMEM(mass_ii.shape, bf16),
-            pltpu.VMEM(mass_bb.shape, bf16),
-            pltpu.VMEM((slots, interior, width + modes), bf16),
-            pltpu.VMEM((slots, interior, 2 * width), bf16),
-            pltpu.VMEM((slots, width, width), f32),
-            pltpu.VMEM((chunks, slots, n_sub, ROWS, cut), f32),
-            pltpu.VMEM((key_rows, lanes), i32),
-            pltpu.VMEM((n_sub, key_rows, lanes), i32),
-            pltpu.VMEM((slots, 2 * NBG * ROWS, lanes), bf16),
-            pltpu.VMEM((chunks, 2 * NBG * ROWS, cut), f32),
-            pltpu.VMEM((places, NBG * ROWS, cut), f32),
-            dma((slots, 5)),
-            dma((chunks, slots)),
-            dma((chunks, slots)),
-            dma,
-            dma,
-            dma((chunks,)),
-            dma((places,)),
-        ],
+        scratch_shapes=scratch,
         compiler_params=pltpu.CompilerParams(
             collective_id=0, has_side_effects=True, vmem_limit_bytes=56 * 1024 * 1024
         ),

time: 34.7 us -> 31.7 us (0.914)
  Pallas kernels: 31.8 us -> 28.8 us
    pallas_call x1, Pallas kernels: 31.8 us -> 28.8 us  [per_device(): pl.pallas_call(functools.partial(body, n_grp, n_sub), out_shape=(pltpu.VM...]
where the time goes in v1:
time: 31.7 us; the launch traced here: 31.5 us
  Pallas kernels  28.8 us (91%)
  local copies, waits for them, and re-layouts  1.45 us (5%)
  between operations  1.29 us (4%)
    pallas_call x1, Pallas kernels, per_device(): pl.pallas_call(functools.partial(body, n_grp, n_sub), out_shape=(pltpu.VM...  28.8 us
    unnamed x2, local copies, waits for them, and re-layouts  1.45 us

profile of v1, /device:TPU:0, one launch (start us, length us, event | category | flops | bytes accessed | tf_op | source)
XLA Modules:
  0.0 31.5 jit_solution(2426284031416434789)
XLA Ops:
  1.3 28.8 %shard_map.95 = (f32[16,16,256]{2,1,0:T(8,128)S(1)}, f32[3,128,256]{2,1,0:T(8,128)S(1)}) custom-call(s32[1]{0:T(128)S(6)} %copy.14.counts, s32[3]{0:T(128)} %codes.1, s32[3,256]{1,0:T(4,128)} %perms.1, bf16[3,1024,1024]{2,1,0:T(8,128)(2,1)} %mass_ii.1, bf16[3,1024,256]{2,1,0:T(8,128)(2,1)} %mass_ib.1, bf16[3,256,256]{2,1,0:T(8,128)(2,1)} %mass_bb.1, ...), custom_call_target="tpu_custom_call" | custom-call | tf_op jit(solution)/shard_map/pallas_call | solution.py:588
  30.1 0.7 %copy.12 = f32[16,16,256]{2,1,0:T(8,128)} copy(f32[16,16,256]{2,1,0:T(8,128)S(1)} %get-tuple-element.2) | data formatting | bytes 524288
  30.8 0.7 %copy.13 = f32[3,128,256]{2,1,0:T(8,128)} copy(f32[3,128,256]{2,1,0:T(8,128)S(1)} %get-tuple-element.3) | data formatting | bytes 786432

commit v2 on v1

--- a/solution.py
+++ b/solution.py
@@ -236,9 +236,9 @@
 def cross_kernel(
     n_grp,
     n_sub,
-    counts,
-    codes,
-    perms,
+    counts_in,
+    codes_in,
+    perms_in,
     mass_ii,
     mass_ib,
     mass_bb,
@@ -246,6 +246,9 @@
     phi_in,
     blocks,
     coupling,
+    counts,
+    codes,
+    perms,
     m_ii,
     m_bb,
     lhs,
@@ -261,6 +264,7 @@
     part,
     passed,
     landed,
+    small_sem,
     in_sem,
     send_sem,
     got_sem,
@@ -274,15 +278,15 @@
     slots, interior, width = psi_in.shape
     own_rows = width // n_sub
     half = n_sub // 2
+    quad = half // 2
     lanes = n_sub * ROWS
     part_rows = NBG * ROWS
     cut = width // 2
-    quad = half // 2
     other = 1 - grp
     spot = lax.rem(me, half)
     first = me - spot
     beyond = half - first
-    twin = beyond + spot
+    corner = lax.rem(me, quad)
     member = grp * half + spot
     reach = grp + me // quad + lax.rem(me // 2, 2)
     gate = jnp.maximum(slots - 1 - reach, 0)
@@ -300,44 +304,34 @@
             for index, (source, into) in enumerate(pairs)
         ]
 
-    for slot in range(slots):
-        for copy in loads(slot):
-            copy.start()
-
+    small = [
+        pltpu.make_async_copy(source, into, small_sem.at[index])
+        for index, (source, into) in enumerate(
+            ((counts_in, counts), (codes_in, codes), (perms_in, perms))
+        )
+    ]
+    for copy in small + loads(0):
+        copy.start()
     def peer_at(base, plane, turn, step):
         low = plane * quad + lax.rem(me + step, quad)
         return lax.rem(grp + turn, n_grp), base + low
 
     steps = [(1, 2), (0, 2), (1, 3), (0, 3), (1, 1), (1, 0), (0, 1), (0, 0)]
-    across = [peer_at(beyond, plane, *step) for plane in range(2) for step in steps]
-    close = [
-        (peer_at(first, plane, *step), None if step != (0, 0) else spot // quad != plane)
-        for plane in range(2)
-        for step in steps
-    ]
+    own_plane = spot // quad
+    across = [[peer_at(beyond, plane, *step) for step in steps] for plane in range(2)]
+    beside = [peer_at(first, own_plane, *step) for step in steps[:-1]]
+    stacked = [peer_at(first, 1 - own_plane, *step) for step in steps]
+    inner = 1 - me // half
+    is_inner = own_plane == inner
+    is_outer = own_plane != inner
+    inward = [peer_at(first, inner, *step) for step in steps]
     barrier = pltpu.get_barrier_semaphore()
 
     def greet(peer):
         pl.semaphore_signal(barrier, inc=1, device_id=peer, device_id_type=MESH)
 
-    def each_close(act):
-        for peer, other_one in close:
-            if other_one is None:
-                act(peer)
-            else:
-                pl.when(other_one)(functools.partial(act, peer))
-
-    for peer in across:
+    for peer in across[0] + across[1] + stacked + beside:
         greet(peer)
-    each_close(greet)
-
-    lane = lax.broadcasted_iota(jnp.int32, (1, lanes), 1)
-    for slot in range(slots):
-        code = codes[slot]
-        block = lax.rem(grp + code // NBG, n_grp) * NBG + lax.rem(code, NBG)
-        block = jnp.where(slot < counts[0], block, -n_grp * NBG) * ROWS
-        key_mine[slot] = jnp.where(lane // ROWS == member, block + lane % ROWS, 0)
-    key_got[0, pl.ds(member, 1)] = key_mine[...][None]
 
     def row_of(peer, owner):
         return pl.multiple_of(owner * own_rows + peer[0] * ROWS, ROWS)
@@ -351,6 +345,15 @@
             device_id=peer,
             device_id_type=MESH,
         ).start()
+
+    def make_keys():
+        lane = lax.broadcasted_iota(jnp.int32, (1, lanes), 1)
+        for slot in range(slots):
+            code = codes[slot]
+            block = lax.rem(grp + code // NBG, n_grp) * NBG + lax.rem(code, NBG)
+            block = jnp.where(slot < counts[0], block, -n_grp * NBG) * ROWS
+            key_mine[slot] = jnp.where(lane // ROWS == member, block + lane % ROWS, 0)
+        key_got[0, pl.ds(member, 1)] = key_mine[...][None]
 
     def send_keys():
         def key_copy(side, peer):
@@ -363,46 +366,68 @@
                 device_id_type=MESH,
             ).start()
 
-        for peer in across:
+        for peer in across[0] + across[1]:
             key_copy(1, peer)
-        each_close(functools.partial(key_copy, 0))
+        for peer in stacked + beside:
+            key_copy(0, peer)
 
     def send_far(slot):
-        for peer in across:
+        for peer in across[1]:
             rows = pl.ds(row_of(peer, peer[1]), ROWS)
-            push(placed.at[slot, rows, pl.ds(0, cut)], far.at[slot, member], 0, slot, peer)
-
-    def held_rows(peer):
-        return pl.ds(row_of(peer, beyond + peer[1] - first), ROWS)
+            push(placed.at[slot, rows, :], far.at[slot, member], 0, slot, peer)
 
     def send_held(slot):
         def one(peer):
-            source = placed.at[slot, held_rows(peer), pl.ds(cut, cut)]
-            push(source, held.at[slot, member], 1, slot, peer)
-
-        each_close(one)
-
-    def send_near(slot):
-        def one(peer):
+            owner = beyond + peer[1] - first - inner * quad
+            rows = pl.ds(row_of(peer, owner), ROWS)
+            push(placed.at[slot, rows, :], held.at[slot, member], 2, slot, peer)
+
+        for peer in inward[:-1]:
+            one(peer)
+        pl.when(is_outer)(functools.partial(one, inward[-1]))
+
+    def send_near(slot, peers):
+        for peer in peers:
             rows = pl.ds(row_of(peer, peer[1]), ROWS)
-            push(placed.at[slot, rows, :], near.at[slot, member], 2, slot, peer)
-
-        each_close(one)
+            push(placed.at[slot, rows, :], near.at[slot, member], 1, slot, peer)
 
     def spread(slot):
+        send_held(slot)
         send_far(slot)
-        send_held(slot)
-        if slot > 0:
-            send_near(slot - 1)
+        if slot == 0:
+            send_keys()
+        send_near(slot, beside)
+
+        @pl.when(is_inner)
+        def outward():
+            send_near(slot, stacked)
+
+        if slot == slots - 1:
+
+            @pl.when(is_outer)
+            def last():
+                for late in range(slots):
+                    send_near(late, stacked)
 
     def reduce_slot(slot):
-        for copy in loads(slot):
+        for copy in loads(slot) + (small if slot == 0 else []):
             copy.wait()
+        if slot + 1 < slots:
+            for copy in loads(slot + 1):
+                copy.start()
         modes = lhs[slot, :, :width]
         step = interior // STRIPS
         for top in range(0, interior, step):
             made = dot(m_ii[slot, top : top + step, :], modes).astype(jnp.bfloat16)
             rhs[slot, top : top + step, :width] = made
+        if slot > 0:
+
+            @pl.when(gate == slot)
+            def enter():
+                pl.semaphore_wait(barrier, 2 * n_sub - 1)
+                for early in range(slot):
+                    spread(early)
+
         every = dot(lhs[slot], rhs[slot], 0, 0)
         cross = every[:width, width:]
         direct = every[:width, :width] + cross + m_bb[slot].astype(jnp.float32)
@@ -418,24 +443,24 @@
         coupling[slot] = (every[width:, :width] + every[width:, width:]) * active
         mine = pl.ds(row_of((grp, me), me), ROWS)
         near[slot, pl.ds(member, 1)] = placed[slot, mine, :][None]
-        mine = pl.ds(row_of((grp, me), twin), ROWS)
-        held[slot, pl.ds(member, 1)] = placed[slot, mine, pl.ds(cut, cut)][None]
+        mine = pl.ds(row_of((grp, me), beyond + corner), ROWS)
+        held[slot, pl.ds(member, 1)] = placed[slot, mine, :][None]
 
     for slot in range(slots):
         reduce_slot(slot)
-
-        @pl.when(gate == slot)
-        def enter():
-            pl.semaphore_wait(barrier, 2 * n_sub - 1)
-            send_keys()
-            for early in range(slot):
-                spread(early)
+        if slot == 0:
+            make_keys()
+
+        if slot == 0:
+
+            @pl.when(gate == slot)
+            def enter():
+                pl.semaphore_wait(barrier, 2 * n_sub - 1)
 
         @pl.when(gate <= slot)
         def follow():
             spread(slot)
 
-    send_near(slots - 1)
 
     many = n_sub - 1
 
@@ -454,67 +479,98 @@
         high, low = split(got.reshape(lanes, got.shape[-1]))
         return dot(hot[side, slot], high) + dot(hot[side, slot], low)
 
-    total = None
-    for slot in range(slots):
-        settle(held.at[slot, pl.ds(0, many)], got_sem.at[1, slot])
-        one = gather(0, slot, held[slot])
-        total = one if total is None else total + one
-    part[...] = total
-
     def hand(to):
         return pltpu.make_async_remote_copy(
             src_ref=part.at[pl.ds(pl.multiple_of(to * part_rows, part_rows), part_rows)],
             dst_ref=landed.at[grp],
             send_sem=pass_send_sem.at[0],
             recv_sem=pass_sem.at[grp],
-            device_id=(to, twin),
+            device_id=(to, beyond + corner),
             device_id_type=MESH,
         )
 
-    hand(other).start()
-    hand(grp).start()
+    @pl.when(is_inner)
+    def fold():
+        total = None
+        for slot in range(slots):
+            settle(held.at[slot, pl.ds(0, many)], got_sem.at[2, slot])
+            one = gather(0, slot, held[slot])
+            total = one if total is None else total + one
+        part[...] = total
+        hand(other).start()
+        hand(grp).start()
+
+    def swap(side):
+        rows = pl.ds(pl.multiple_of(other * part_rows, part_rows), part_rows)
+        return pltpu.make_async_remote_copy(
+            src_ref=sums.at[side, rows],
+            dst_ref=passed.at[side],
+            send_sem=pass_send_sem.at[1 + side],
+            recv_sem=pass_sem.at[n_grp + side],
+            device_id=(other, me),
+            device_id_type=MESH,
+        )
 
     total = None
     for slot in range(slots):
-        settle(near.at[slot, pl.ds(0, many)], got_sem.at[2, slot])
+        settle(near.at[slot, pl.ds(0, many)], got_sem.at[1, slot])
         one = gather(0, slot, near[slot])
         total = one if total is None else total + one
-    sums[...] = total
-    total = None
-    for slot in range(slots):
-        settle(far.at[slot], got_sem.at[0, slot])
-        one = gather(1, slot, far[slot])
-        total = one if total is None else total + one
-    sums[:, :cut] = sums[:, :cut] + total
-    swap = pltpu.make_async_remote_copy(
-        src_ref=sums.at[pl.ds(pl.multiple_of(other * part_rows, part_rows), part_rows)],
-        dst_ref=passed,
-        send_sem=pass_send_sem.at[1],
-        recv_sem=pass_sem.at[2],
-        device_id=(other, me),
-        device_id_type=MESH,
-    )
-    swap.start()
+    for side in range(2):
+        sums[side] = total[:, side * cut : (side + 1) * cut]
+
+    @pl.when(own_plane == 1)
+    def direct():
+        total = None
+        for slot in range(slots):
+            settle(far.at[slot], got_sem.at[0, slot])
+            one = gather(1, slot, far[slot])
+            total = one if total is None else total + one
+        for side in range(2):
+            sums[side] = sums[side] + total[:, side * cut : (side + 1) * cut]
+
+    for side in range(2):
+        swap(side).start()
 
     settle(key_got.at[0, pl.ds(0, many)], key_send_sem.at[0])
     settle(key_got.at[1], key_send_sem.at[1])
     for slot in range(slots):
-        settle(far.at[slot], send_sem.at[0, slot])
-        settle(held.at[slot, pl.ds(0, many)], send_sem.at[1, slot])
-        settle(near.at[slot, pl.ds(0, many)], send_sem.at[2, slot])
-
-    kept = sums[pl.ds(pl.multiple_of(grp * part_rows, part_rows), part_rows), :]
-    swap.wait()
-    for row, value in ((grp, kept), (other, passed[...])):
+        settle(far.at[slot, pl.ds(0, len(steps))], send_sem.at[0, slot])
+        settle(near.at[slot, pl.ds(0, many)], send_sem.at[1, slot])
+        settle(held.at[slot, pl.ds(0, len(steps) - 1)], send_sem.at[2, slot])
+
+    @pl.when(is_outer)
+    def sent():
+        for slot in range(slots):
+            settle(held.at[slot, pl.ds(0, 1)], send_sem.at[2, slot])
+
+    mine = pl.ds(pl.multiple_of(grp * part_rows, part_rows), part_rows)
+    def put(row, side, value):
         into = pl.ds(pl.multiple_of(row * ROWS, ROWS), ROWS)
-        blocks[:, into, :cut] = value[:, :cut].reshape(NBG, ROWS, cut)
-    settle(landed.at[0], pass_sem.at[0])
-    settle(landed.at[1], pass_sem.at[1])
-    for row, value in ((grp, kept), (other, passed[...])):
-        into = pl.ds(pl.multiple_of(row * ROWS, ROWS), ROWS)
-        late = value[:, cut:] + landed[row]
-        blocks[:, into, cut:] = late.reshape(NBG, ROWS, cut)
-    settle(landed, pass_send_sem.at[0])
+        blocks[:, into, side * cut : (side + 1) * cut] = value.reshape(NBG, ROWS, cut)
+
+    @pl.when(own_plane == 1)
+    def finish():
+        for side in range(2):
+            put(grp, side, sums[side, mine, :])
+        for side in range(2):
+            swap(side).wait()
+            put(other, side, passed[side])
+
+    @pl.when(own_plane == 0)
+    def finish_landed():
+        for side in range(2):
+            swap(side).wait()
+        for place in range(n_grp):
+            settle(landed.at[place], pass_sem.at[place])
+        for side in range(2):
+            columns = slice(side * cut, (side + 1) * cut)
+            put(grp, side, sums[side, mine, :] + landed[grp][:, columns])
+            put(other, side, passed[side] + landed[other][:, columns])
+
+    @pl.when(is_inner)
+    def handed():
+        settle(part, pass_send_sem.at[0])
 
 
 def cross_scratch(n_grp, n_sub, slots, interior, width, modes):
@@ -523,28 +579,32 @@
     lanes, cut = n_sub * ROWS, width // 2
     total = n_grp * NBG * ROWS
     return [
+        pltpu.SMEM((1,), i32),
+        pltpu.SMEM((slots,), i32),
+        pltpu.VMEM((slots, width), i32),
         pltpu.VMEM((slots, interior, interior), bf16),
         pltpu.VMEM((slots, width, width), bf16),
         pltpu.VMEM((slots, interior, width + modes), bf16),
         pltpu.VMEM((slots, interior, 2 * width), bf16),
         pltpu.VMEM((slots, width, width), f32),
         pltpu.VMEM((slots, n_sub, ROWS, width), f32),
-        pltpu.VMEM((slots, n_sub, ROWS, cut), f32),
-        pltpu.VMEM((slots, n_sub, ROWS, cut), f32),
+        pltpu.VMEM((slots, n_sub, ROWS, width), f32),
+        pltpu.VMEM((slots, n_sub, ROWS, width), f32),
         pltpu.VMEM((slots, 1, lanes), i32),
         pltpu.VMEM((2, n_sub, slots, 1, lanes), i32),
         pltpu.VMEM((2, slots, total, lanes), bf16),
+        pltpu.VMEM((2, total, cut), f32),
         pltpu.VMEM((total, width), f32),
-        pltpu.VMEM((total, cut), f32),
-        pltpu.VMEM((NBG * ROWS, width), f32),
-        pltpu.VMEM((n_grp, NBG * ROWS, cut), f32),
+        pltpu.VMEM((2, NBG * ROWS, cut), f32),
+        pltpu.VMEM((n_grp, NBG * ROWS, width), f32),
+        dma((3,)),
         dma((slots, 5)),
         dma((3, slots)),
         dma((3, slots)),
         dma((2,)),
         dma((2,)),
-        dma((2,)),
         dma((3,)),
+        dma((n_grp + 2,)),
     ]
 
 
@@ -560,6 +620,7 @@
     smem = pl.BlockSpec(memory_space=pltpu.SMEM)
     vmem = pl.BlockSpec(memory_space=pltpu.VMEM)
     hbm = pl.BlockSpec(memory_space=pl.ANY)
+    vmem_in = vmem
     bf16, f32, i32 = jnp.bfloat16, jnp.float32, jnp.int32
     dma = pltpu.SemaphoreType.DMA
     scratch = [
@@ -583,7 +644,7 @@
         dma((chunks,)),
     ]
     if fits and interior % STRIPS == 0:
-        body = cross_kernel
+        body, smem, vmem_in = cross_kernel, hbm, hbm
         scratch = cross_scratch(n_grp, n_sub, slots, interior, width, modes)
     return pl.pallas_call(
         functools.partial(body, n_grp, n_sub),
@@ -591,7 +652,7 @@
             pltpu.VMEM((NBG, own_rows, width), f32),
             pltpu.VMEM((slots, modes, width), f32),
         ),
-        in_specs=[smem, smem, vmem] + [hbm] * 5,
+        in_specs=[smem, smem, vmem_in] + [hbm] * 5,
         out_specs=(vmem, vmem),
         scratch_shapes=scratch,
         compiler_params=pltpu.CompilerParams(

time: 31.7 us -> 30.4 us (0.959)
  the two profiles are of different devices: /device:TPU:0 before, /device:TPU:17 now
where the time goes in v2:
time: 30.4 us; the launch traced here: 30.2 us
  Pallas kernels  27.5 us (90%)
  local copies, waits for them, and re-layouts  1.45 us (5%)
  between operations  1.29 us (4%)
    pallas_call x1, Pallas kernels, per_device(): pl.pallas_call(functools.partial(body, n_grp, n_sub), out_shape=(pltpu.VM...  27.5 us
    unnamed x2, local copies, waits for them, and re-layouts  1.45 us

profile of v2, /device:TPU:17, one launch (start us, length us, event | category | flops | bytes accessed | tf_op | source)
XLA Modules:
  0.0 30.2 jit_solution(17722351285834568536)
XLA Ops:
  1.3 27.5 %shard_map.95 = (f32[16,16,256]{2,1,0:T(8,128)S(1)}, f32[3,128,256]{2,1,0:T(8,128)S(1)}) custom-call(s32[1]{0:T(128)S(6)} %copy.14.counts_in, s32[3]{0:T(128)} %codes_in.1, s32[3,256]{1,0:T(4,128)} %perms_in.1, bf16[3,1024,1024]{2,1,0:T(8,128)(2,1)} %mass_ii.1, bf16[3,1024,256]{2,1,0:T(8,128)(2,1)} %mass_ib.1, bf16[3,256,256]{2,1,0:T(8,128)(2,1)} %mass_bb.1, ...), custom_call_target="tpu_custom_call" | custom-call | tf_op jit(solution)/shard_map/pallas_call | solution.py:649
  28.8 0.7 %copy.12 = f32[16,16,256]{2,1,0:T(8,128)} copy(f32[16,16,256]{2,1,0:T(8,128)S(1)} %get-tuple-element.2) | data formatting | bytes 524288
  29.5 0.7 %copy.13 = f32[3,128,256]{2,1,0:T(8,128)} copy(f32[3,128,256]{2,1,0:T(8,128)S(1)} %get-tuple-element.3) | data formatting | bytes 786432

commit v3 on v2

--- a/solution.py
+++ b/solution.py
@@ -324,6 +324,7 @@
     inner = 1 - me // half
     is_inner = own_plane == inner
     is_outer = own_plane != inner
+    prompt = own_plane + first > 0
     inward = [peer_at(first, inner, *step) for step in steps]
     barrier = pltpu.get_barrier_semaphore()
 
@@ -348,12 +349,14 @@
 
     def make_keys():
         lane = lax.broadcasted_iota(jnp.int32, (1, lanes), 1)
+        row = jnp.zeros((1, lanes), jnp.int32)
         for slot in range(slots):
             code = codes[slot]
             block = lax.rem(grp + code // NBG, n_grp) * NBG + lax.rem(code, NBG)
-            block = jnp.where(slot < counts[0], block, -n_grp * NBG) * ROWS
-            key_mine[slot] = jnp.where(lane // ROWS == member, block + lane % ROWS, 0)
-        key_got[0, pl.ds(member, 1)] = key_mine[...][None]
+            block = jnp.where(slot < counts[0], block, -n_grp * NBG)
+            row = row + jnp.where(lane == member * ROWS + slot, block, 0)
+        key_mine[...] = row
+        key_got[0, pl.ds(member, 1)] = row[None]
 
     def send_keys():
         def key_copy(side, peer):
@@ -386,28 +389,44 @@
             one(peer)
         pl.when(is_outer)(functools.partial(one, inward[-1]))
 
-    def send_near(slot, peers):
+    def send_near(slot, side, peers):
         for peer in peers:
             rows = pl.ds(row_of(peer, peer[1]), ROWS)
-            push(placed.at[slot, rows, :], near.at[slot, member], 1, slot, peer)
+            source = placed.at[slot, rows, pl.ds(side * cut, cut)]
+            push(source, near.at[side, slot, member], 1 + 2 * side, slot, peer)
 
     def spread(slot):
         send_held(slot)
-        send_far(slot)
+
+        @pl.when(prompt)
+        def at_once():
+            send_far(slot)
+
+        if slot > 0:
+
+            @pl.when(jnp.logical_not(prompt))
+            def one_late():
+                send_far(slot - 1)
+                if slot == slots - 1:
+                    send_far(slot)
+
         if slot == 0:
             send_keys()
-        send_near(slot, beside)
+        for side in (1, 0):
+            send_near(slot, side, beside)
 
         @pl.when(is_inner)
         def outward():
-            send_near(slot, stacked)
+            for side in (1, 0):
+                send_near(slot, side, stacked)
 
         if slot == slots - 1:
 
             @pl.when(is_outer)
             def last():
-                for late in range(slots):
-                    send_near(late, stacked)
+                for side in (1, 0):
+                    for late in range(slots):
+                        send_near(late, side, stacked)
 
     def reduce_slot(slot):
         for copy in loads(slot) + (small if slot == 0 else []):
@@ -442,7 +461,9 @@
         active = jnp.where(slot < counts[0], 1.0, 0.0)
         coupling[slot] = (every[width:, :width] + every[width:, width:]) * active
         mine = pl.ds(row_of((grp, me), me), ROWS)
-        near[slot, pl.ds(member, 1)] = placed[slot, mine, :][None]
+        for side in range(2):
+            own = placed[slot, mine, side * cut : (side + 1) * cut]
+            near[side, slot, pl.ds(member, 1)] = own[None]
         mine = pl.ds(row_of((grp, me), beyond + corner), ROWS)
         held[slot, pl.ds(member, 1)] = placed[slot, mine, :][None]
 
@@ -470,10 +491,18 @@
     settle(key_got.at[0, pl.ds(0, many)], key_sem.at[0])
     settle(key_got.at[1], key_sem.at[1])
     target = lax.broadcasted_iota(jnp.int32, (n_grp * part_rows, lanes), 0)
+    target = target.astype(jnp.float32)
+    source = lax.broadcasted_iota(jnp.int32, (lanes, lanes), 0)
+    lane = lax.broadcasted_iota(jnp.int32, (lanes, lanes), 1)
+    lead = lane - lane % ROWS
+    within = (lane[:1] % ROWS).astype(jnp.float32)
     for side in range(2):
-        keys = jnp.sum(key_got[side], axis=0)
+        keys = jnp.sum(key_got[side], axis=0).astype(jnp.float32)
+        keys = jnp.broadcast_to(keys, (ROWS, lanes)).astype(jnp.bfloat16)
         for slot in range(slots):
-            hot[side, slot] = jnp.where(target == keys[slot], 1.0, 0.0).astype(jnp.bfloat16)
+            move = jnp.where(source == lead + slot, 1.0, 0.0).astype(jnp.bfloat16)
+            key = dot(keys, move)[:1] * ROWS + within
+            hot[side, slot] = jnp.where(target == key, 1.0, 0.0).astype(jnp.bfloat16)
 
     def gather(side, slot, got):
         high, low = split(got.reshape(lanes, got.shape[-1]))
@@ -511,13 +540,16 @@
             device_id_type=MESH,
         )
 
-    total = None
-    for slot in range(slots):
-        settle(near.at[slot, pl.ds(0, many)], got_sem.at[1, slot])
-        one = gather(0, slot, near[slot])
-        total = one if total is None else total + one
-    for side in range(2):
-        sums[side] = total[:, side * cut : (side + 1) * cut]
+    def near_sum(side):
+        total = None
+        for slot in range(slots):
+            settle(near.at[side, slot, pl.ds(0, many)], got_sem.at[1 + 2 * side, slot])
+            one = gather(0, slot, near[side, slot])
+            total = one if total is None else total + one
+        return total
+
+    sums[0] = jnp.zeros_like(sums[0])
+    sums[1] = near_sum(1)
 
     @pl.when(own_plane == 1)
     def direct():
@@ -526,17 +558,19 @@
             settle(far.at[slot], got_sem.at[0, slot])
             one = gather(1, slot, far[slot])
             total = one if total is None else total + one
-        for side in range(2):
-            sums[side] = sums[side] + total[:, side * cut : (side + 1) * cut]
-
-    for side in range(2):
-        swap(side).start()
+        sums[1] = sums[1] + total[:, cut:]
+        sums[0] = total[:, :cut]
+
+    swap(1).start()
+    sums[0] = sums[0] + near_sum(0)
+    swap(0).start()
 
     settle(key_got.at[0, pl.ds(0, many)], key_send_sem.at[0])
     settle(key_got.at[1], key_send_sem.at[1])
     for slot in range(slots):
         settle(far.at[slot, pl.ds(0, len(steps))], send_sem.at[0, slot])
-        settle(near.at[slot, pl.ds(0, many)], send_sem.at[1, slot])
+        for side in range(2):
+            settle(near.at[side, slot, pl.ds(0, many)], send_sem.at[1 + 2 * side, slot])
         settle(held.at[slot, pl.ds(0, len(steps) - 1)], send_sem.at[2, slot])
 
     @pl.when(is_outer)
@@ -553,17 +587,16 @@
     def finish():
         for side in range(2):
             put(grp, side, sums[side, mine, :])
-        for side in range(2):
+        for side in (1, 0):
             swap(side).wait()
             put(other, side, passed[side])
 
     @pl.when(own_plane == 0)
     def finish_landed():
-        for side in range(2):
-            swap(side).wait()
         for place in range(n_grp):
             settle(landed.at[place], pass_sem.at[place])
-        for side in range(2):
+        for side in (1, 0):
+            swap(side).wait()
             columns = slice(side * cut, (side + 1) * cut)
             put(grp, side, sums[side, mine, :] + landed[grp][:, columns])
             put(other, side, passed[side] + landed[other][:, columns])
@@ -587,11 +620,11 @@
         pltpu.VMEM((slots, interior, width + modes), bf16),
         pltpu.VMEM((slots, interior, 2 * width), bf16),
         pltpu.VMEM((slots, width, width), f32),
+        pltpu.VMEM((2, slots, n_sub, ROWS, cut), f32),
         pltpu.VMEM((slots, n_sub, ROWS, width), f32),
         pltpu.VMEM((slots, n_sub, ROWS, width), f32),
-        pltpu.VMEM((slots, n_sub, ROWS, width), f32),
-        pltpu.VMEM((slots, 1, lanes), i32),
-        pltpu.VMEM((2, n_sub, slots, 1, lanes), i32),
+        pltpu.VMEM((1, lanes), i32),
+        pltpu.VMEM((2, n_sub, 1, lanes), i32),
         pltpu.VMEM((2, slots, total, lanes), bf16),
         pltpu.VMEM((2, total, cut), f32),
         pltpu.VMEM((total, width), f32),
@@ -599,8 +632,8 @@
         pltpu.VMEM((n_grp, NBG * ROWS, width), f32),
         dma((3,)),
         dma((slots, 5)),
-        dma((3, slots)),
-        dma((3, slots)),
+        dma((4, slots)),
+        dma((4, slots)),
         dma((2,)),
         dma((2,)),
         dma((3,)),
@@ -643,7 +676,7 @@
         dma((chunks,)),
         dma((chunks,)),
     ]
-    if fits and interior % STRIPS == 0:
+    if fits and interior % STRIPS == 0 and slots <= ROWS:
         body, smem, vmem_in = cross_kernel, hbm, hbm
         scratch = cross_scratch(n_grp, n_sub, slots, interior, width, modes)
     return pl.pallas_call(

time: 30.4 us -> 29.2 us (0.961)
  the two profiles are of different devices: /device:TPU:17 before, /device:TPU:0 now
where the time goes in v3:
time: 29.2 us; the launch traced here: 29 us
  Pallas kernels  26.3 us (90%)
  local copies, waits for them, and re-layouts  1.45 us (5%)
  between operations  1.29 us (4%)
    pallas_call x1, Pallas kernels, per_device(): pl.pallas_call(functools.partial(body, n_grp, n_sub), out_shape=(pltpu.VM...  26.3 us
    unnamed x2, local copies, waits for them, and re-layouts  1.45 us

profile of v3, /device:TPU:0, one launch (start us, length us, event | category | flops | bytes accessed | tf_op | source)
XLA Modules:
  0.0 29.0 jit_solution(8620054370446805565)
XLA Ops:
  1.3 26.3 %shard_map.95 = (f32[16,16,256]{2,1,0:T(8,128)S(1)}, f32[3,128,256]{2,1,0:T(8,128)S(1)}) custom-call(s32[1]{0:T(128)S(6)} %copy.14.counts_in, s32[3]{0:T(128)} %codes_in.1, s32[3,256]{1,0:T(4,128)} %perms_in.1, bf16[3,1024,1024]{2,1,0:T(8,128)(2,1)} %mass_ii.1, bf16[3,1024,256]{2,1,0:T(8,128)(2,1)} %mass_ib.1, bf16[3,256,256]{2,1,0:T(8,128)(2,1)} %mass_bb.1, ...), custom_call_target="tpu_custom_call" | custom-call | tf_op jit(solution)/shard_map/pallas_call | solution.py:682
  27.6 0.7 %copy.12 = f32[16,16,256]{2,1,0:T(8,128)} copy(f32[16,16,256]{2,1,0:T(8,128)S(1)} %get-tuple-element.2) | data formatting | bytes 524288
  28.3 0.7 %copy.13 = f32[3,128,256]{2,1,0:T(8,128)} copy(f32[3,128,256]{2,1,0:T(8,128)S(1)} %get-tuple-element.3) | data formatting | bytes 786432

commit v4 on v3

--- a/solution.py
+++ b/solution.py
@@ -289,7 +289,7 @@
     corner = lax.rem(me, quad)
     member = grp * half + spot
     reach = grp + me // quad + lax.rem(me // 2, 2)
-    gate = jnp.maximum(slots - 1 - reach, 0)
+    gate = jnp.where(reach < 2, 1, 0)
 
     def loads(slot):
         pairs = (
@@ -396,37 +396,24 @@
             push(source, near.at[side, slot, member], 1 + 2 * side, slot, peer)
 
     def spread(slot):
-        send_held(slot)
-
-        @pl.when(prompt)
-        def at_once():
-            send_far(slot)
-
-        if slot > 0:
-
-            @pl.when(jnp.logical_not(prompt))
-            def one_late():
-                send_far(slot - 1)
-                if slot == slots - 1:
-                    send_far(slot)
-
-        if slot == 0:
-            send_keys()
-        for side in (1, 0):
-            send_near(slot, side, beside)
-
-        @pl.when(is_inner)
-        def outward():
-            for side in (1, 0):
-                send_near(slot, side, stacked)
-
-        if slot == slots - 1:
-
-            @pl.when(is_outer)
-            def last():
-                for side in (1, 0):
-                    for late in range(slots):
-                        send_near(late, side, stacked)
+        def run(words):
+            for word in words:
+                kind, at = word[0], int(word[1])
+                if kind == "h":
+                    send_held(at)
+                if kind == "f":
+                    send_far(at)
+                if kind == "s":
+                    send_near(at % 3, 1 if at < 3 else 0, stacked)
+                if kind == "b":
+                    send_near(at, 1, beside)
+                    send_near(at, 0, beside)
+                if kind == "k":
+                    send_keys()
+
+        pl.when(is_inner)(functools.partial(run, [['h0', 'f0', 'k0', 's0', 's3', 'b0'], ['h1', 'f1', 's1', 's4', 'b1'], ['h2', 'f2', 's2', 's5', 'b2']][slot]))
+        pl.when(own_plane + first == 0)(functools.partial(run, [['h0', 'k0', 'b0'], ['h1', 'f0', 'b1'], ['h2', 'f1', 'f2', 'b2', 's0', 's1', 's2', 's3', 's4', 's5']][slot]))
+        pl.when(own_plane * first == half)(functools.partial(run, [['h0', 'f0', 'k0', 'b0'], ['h1', 'f1', 'b1'], ['h2', 'b2', 's0', 's1', 's2', 'f2', 's3', 's4', 's5']][slot]))
 
     def reduce_slot(slot):
         for copy in loads(slot) + (small if slot == 0 else []):
@@ -526,8 +513,9 @@
             one = gather(0, slot, held[slot])
             total = one if total is None else total + one
         part[...] = total
-        hand(other).start()
-        hand(grp).start()
+        early = jnp.where(first > 0, 0, other)
+        hand(early).start()
+        hand(1 - early).start()
 
     def swap(side):
         rows = pl.ds(pl.multiple_of(other * part_rows, part_rows), part_rows)
@@ -676,7 +664,7 @@
         dma((chunks,)),
         dma((chunks,)),
     ]
-    if fits and interior % STRIPS == 0 and slots <= ROWS:
+    if fits and interior % STRIPS == 0 and slots == 3:
         body, smem, vmem_in = cross_kernel, hbm, hbm
         scratch = cross_scratch(n_grp, n_sub, slots, interior, width, modes)
     return pl.pallas_call(

time: 29.2 us -> 28.5 us (0.976)
  the two profiles are of different devices: /device:TPU:0 before, /device:TPU:17 now
where the time goes in v4:
time: 28.5 us; the launch traced here: 28.3 us
  Pallas kernels  25.6 us (90%)
  local copies, waits for them, and re-layouts  1.45 us (5%)
  between operations  1.29 us (5%)
    pallas_call x1, Pallas kernels, per_device(): pl.pallas_call(functools.partial(body, n_grp, n_sub), out_shape=(pltpu.VM...  25.6 us
    unnamed x2, local copies, waits for them, and re-layouts  1.45 us

profile of v4, /device:TPU:17, one launch (start us, length us, event | category | flops | bytes accessed | tf_op | source)
XLA Modules:
  0.0 28.3 jit_solution(16749678919467979442)
XLA Ops:
  1.3 25.6 %shard_map.95 = (f32[16,16,256]{2,1,0:T(8,128)S(1)}, f32[3,128,256]{2,1,0:T(8,128)S(1)}) custom-call(s32[1]{0:T(128)S(6)} %copy.14.counts_in, s32[3]{0:T(128)} %codes_in.1, s32[3,256]{1,0:T(4,128)} %perms_in.1, bf16[3,1024,1024]{2,1,0:T(8,128)(2,1)} %mass_ii.1, bf16[3,1024,256]{2,1,0:T(8,128)(2,1)} %mass_ib.1, bf16[3,256,256]{2,1,0:T(8,128)(2,1)} %mass_bb.1, ...), custom_call_target="tpu_custom_call" | custom-call | tf_op jit(solution)/shard_map/pallas_call | solution.py:670
  26.9 0.7 %copy.12 = f32[16,16,256]{2,1,0:T(8,128)} copy(f32[16,16,256]{2,1,0:T(8,128)S(1)} %get-tuple-element.2) | data formatting | bytes 524288
  27.6 0.7 %copy.13 = f32[3,128,256]{2,1,0:T(8,128)} copy(f32[3,128,256]{2,1,0:T(8,128)S(1)} %get-tuple-element.3) | data formatting | bytes 786432
